TPU v7x, 32 devices: a whole 2x2x4 slice. The times are simulated.
32 devices in a mesh: rows: 4 (over y, x), mp: 8 (over z, core).
Axes of the slice: x: 2, y: 2, z: 4, core: 2. Of those that a mesh axis runs over, the one named last changes fastest.
Arguments:
- tokens: bfloat16 [512, 6144], P('rows', 'mp'), may hold values from -8 to 8
- norm_gain: float32 [6144], replicated, may hold values from 0.25 to 1.75
- hidden_bias: float32 [24576], P('mp'), may hold values from -3 to 3
- weight_in: bfloat16 [6144, 24576], P('rows', 'mp'), may hold values from -0.078125 to 0.078125
- weight_out: bfloat16 [24576, 6144], P('mp', 'rows'), may hold values from -0.0546875 to 0.0546875
Outputs:
- updated: bfloat16 [512, 6144], P('rows', 'mp')
All inputs are finite; a program needn't handle non-finite values.
Results may differ from a plain program's by a relative error of at most 0.0041.
Values may be sent and summed in bfloat16 or wider, within the bound.
A program may use at most 128 MiB of HBM per device.

v0:
```python
import jax
import jax.numpy as jnp
from jax import lax
from jax.sharding import PartitionSpec as P

D = 6144
floor_value = 0.1


def normalize(as_float, moment_sum, square_sum, gain, width):
    row_mean = moment_sum / width
    row_var = jnp.maximum(square_sum / width - row_mean * row_mean, 0.0)
    inverse = lax.rsqrt(row_var + floor_value)
    return ((as_float - row_mean[:, None]) * inverse[:, None] * gain[None, :]).astype(jnp.bfloat16)


def body(tokens, norm_gain, hidden_bias, weight_in, weight_out):
    as_float = tokens.astype(jnp.float32)
    moment_sum, square_sum = lax.psum(
        (jnp.sum(as_float, axis=1), jnp.sum(as_float * as_float, axis=1)), "mp"
    )
    local_gain = lax.dynamic_slice_in_dim(
        norm_gain, lax.axis_index("mp") * tokens.shape[1], tokens.shape[1]
    )
    shard_norm = normalize(as_float, moment_sum, square_sum, local_gain, D)
    normed = lax.all_gather(shard_norm, "mp", axis=1, tiled=True)
    shuffled = lax.all_to_all(normed, "rows", split_axis=1, concat_axis=0, tiled=True)
    preact = lax.psum_scatter(
        jnp.dot(shuffled, weight_in, preferred_element_type=jnp.float32),
        "rows",
        scatter_dimension=0,
        tiled=True,
    )
    hidden = jax.nn.gelu(preact + hidden_bias[None, :], approximate=False).astype(jnp.bfloat16)
    terms = jnp.dot(
        hidden,
        lax.all_gather(weight_out, "rows", axis=1, tiled=True),
        preferred_element_type=jnp.float32,
    )
    branch = lax.psum_scatter(terms, "mp", scatter_dimension=1, tiled=True)
    return (as_float + branch).astype(jnp.bfloat16)


def solution(mesh):
    return jax.shard_map(
        body,
        mesh=mesh,
        in_specs=(P("rows", "mp"), P(), P("mp"), P("rows", "mp"), P("mp", "rows")),
        out_specs=P("rows", "mp"),
        check_vma=False,
    )
```

profile of v0, /device:TPU:0, one launch (start us, length us, event | category | flops | bytes accessed | tf_op | source)
XLA Modules:
  0.0 561.1 jit_solution(460465434844182383)
XLA Ops:
  6.5 0.0 all-gather.3.cloned.1.call-start
  6.5 1.1 convert_reduce_fusion
  7.6 18.1 %all-reduce = (f32[128]{0:T(128)S(1)}, f32[128]{0:T(128)S(1)}) all-reduce(f32[128]{0:T(128)S(1)} %get-tuple-element.6, f32[128]{0:T(128)S(1)} %get-tuple-element.5), channel_id=1, replica_groups=mesh['rows'=4,'mp'=8] {'mp'}, use_global_device_ids=true, to_apply=%region_3.0 | all-reduce | flops 256 | bytes 2048 | tf_op jit(solution)/shard_map/psum | solution.py:19
  25.7 0.8 dynamic_slice.3
  26.5 1.8 fusion.45
  28.3 0.0 all-gather.3.cloned.1.call-update
  28.3 0.0 reduce-scatter.3.cloned.1.call-start
  28.3 23.6 %all-gather.3.cloned.1.call-done = bf16[128,6144]{1,0:T(8,128)(2,1)} async-done(((bf16[128,768]{1,0:T(8,128)(2,1)}), bf16[128,6144]{1,0:T(8,128)(2,1)}) %all-gather.3.cloned.1.call-update) | async-done | bytes 1572880 | tf_op jit(solution)/shard_map/all_gather | solution.py:26
  51.9 1.5 copy.9
  53.4 23.6 %all_to_all.19 = bf16[128,4,1536]{2,0,1:T(8,128)(2,1)S(1)} all-to-all(bf16[128,4,1536]{2,0,1:T(8,128)(2,1)S(1)} %bitcast.10), channel_id=1, replica_groups=mesh['rows'=4,'mp'=8] {'rows'}, dimensions={1} | all-to-all | bytes 3145728 | tf_op jit(solution)/shard_map/all_to_all | solution.py:27
  77.0 10.6 %fusion.78 = f32[512,3072]{1,0:T(8,128)} fusion(bf16[512,1536]{1,0:T(8,128)(2,1)S(1)} %bitcast.12, bf16[1536,3072]{1,0:T(8,128)(2,1)} %param.8), kind=kOutput, calls=%fused_computation.93 | convolution fusion | flops 4831838208 | bytes 17301504 | tf_op jit(solution)/shard_map/dot_general | solution.py:29
  87.6 0.0 reduce-scatter.3.cloned.1.call-update
  87.6 0.0 copy-start.1
  87.6 0.0 all-gather.5.cloned.1.call-start
  87.7 0.7 all-gather.5.cloned.1.call-update
  88.4 0.0 reduce-scatter.5.cloned.1.call-start
  88.4 67.0 %reduce-scatter.3.cloned.1.call-done = f32[128,3072]{1,0:T(8,128)} async-done(((f32[512,3072]{1,0:T(8,128)}), f32[128,3072]{1,0:T(8,128)}) %reduce-scatter.3.cloned.1.call-update) | async-done | bytes 1572880 | tf_op jit(solution)/shard_map/reduce_scatter | solution.py:28
  155.5 334.7 %all-gather.5.cloned.1.call-done = bf16[3072,6144]{1,0:T(8,128)(2,1)} async-done(((bf16[3072,1536]{1,0:T(8,128)(2,1)}), bf16[3072,6144]{1,0:T(8,128)(2,1)}) %all-gather.5.cloned.1.call-update) | async-done | bytes 37748752 | tf_op jit(solution)/shard_map/all_gather | solution.py:37
  490.2 0.0 copy-done.1
  490.2 22.1 %fusion.10 = f32[128,6144]{1,0:T(8,128)} fusion(bf16[3072,6144]{1,0:T(8,128)(2,1)} %all-gather.5.cloned.1.call-done, f32[128,3072]{1,0:T(8,128)} %reduce-scatter.3.cloned.1.call-done, f32[3072]{0:T(1024)S(1)} %copy-done.1), kind=kOutput, calls=%fused_computation.20 | convolution fusion | flops 4857790464 | bytes 42479616 | tf_op jit(solution)/shard_map/dot_general | solution.py:35
  512.3 0.0 copy-start
  512.3 0.0 reduce-scatter.5.cloned.1.call-update
  512.3 40.5 %reduce-scatter.5.cloned.1.call-done = f32[128,768]{1,0:T(8,128)} async-done(((f32[128,6144]{1,0:T(8,128)}), f32[128,768]{1,0:T(8,128)}) %reduce-scatter.5.cloned.1.call-update) | async-done | bytes 393232 | tf_op jit(solution)/shard_map/reduce_scatter | solution.py:40
  552.8 0.0 copy-done
  552.8 1.7 fusion.47
  (1 shorter events, 0.0 us)
Async XLA Ops:
  6.5 45.4 %all-gather.3.cloned.1.call-start = ((), (), s32[]{:S(2)}) async-start(), calls=%async_computation.3 | async-start | bytes 1769472 | tf_op jit(solution)/shard_map/all_gather | solution.py:26
  28.3 127.2 %reduce-scatter.3.cloned.1.call-start = ((), (), s32[]{:S(2)}) async-start(), calls=%async_computation.4 | async-start | bytes 7864320 | tf_op jit(solution)/shard_map/reduce_scatter | solution.py:28
  87.6 402.6 %copy-start.1 = (f32[3072]{0:T(1024)S(1)}, f32[3072]{0:T(1024)}, u32[]{:S(2)}) copy-start(f32[3072]{0:T(1024)} %param.7) | copy-start | bytes 36868
  87.6 402.6 %all-gather.5.cloned.1.call-start = ((), (), s32[]{:S(2)}) async-start(), calls=%async_computation.5 | async-start | bytes 47185920 | tf_op jit(solution)/shard_map/all_gather | solution.py:37
  88.4 464.4 %reduce-scatter.5.cloned.1.call-start = ((), (), s32[]{:S(2)}) async-start(), calls=%async_computation.6 | async-start | bytes 3538944 | tf_op jit(solution)/shard_map/reduce_scatter | solution.py:40
  512.3 40.6 %copy-start = (bf16[128,768]{1,0:T(8,128)(2,1)S(1)}, bf16[128,768]{1,0:T(8,128)(2,1)}, u32[]{:S(2)}) copy-start(bf16[128,768]{1,0:T(8,128)(2,1)} %param.5) | copy-start | bytes 589828
Sparse Core Ops, SparseCore 0:
  28.4 23.4 all-gather.2
  87.7 67.6 reduce-scatter.2
  157.3 332.8 all-gather.4
  512.4 40.3 reduce-scatter.4
where the time goes:
time: 561 us
  waiting for transfers between devices  467 us (83%)
  blocking collectives  41.7 us (7%)
  matrix products  32.6 us (6%)
  between operations  13.2 us (2%)
    all_gather x1, waiting for transfers between devices, body(): lax.all_gather(weight_out, 'rows', axis=1, tiled=True)  335 us
    reduce_scatter x1, waiting for transfers between devices, body(): lax.psum_scatter(jnp.dot(shuffled, weight_in, preferred_element_type=jnp....  67 us
    reduce_scatter x1, waiting for transfers between devices, body(): branch = lax.psum_scatter(terms, 'mp', scatter_dimension=1, tiled=True)  40.5 us
    all_to_all x1, blocking collectives, body(): lax.all_to_all(normed, 'rows', split_axis=1, concat_axis=0, tiled=True)  23.6 us
    all_gather x1, waiting for transfers between devices, body(): normed = lax.all_gather(shard_norm, 'mp', axis=1, tiled=True)  23.6 us
    dot_general x1, matrix products, body(): jnp.dot(hidden, lax.all_gather(weight_out, 'rows', axis=1, tiled=True), p...  22.1 us
    psum x1, blocking collectives, body(): lax.psum((jnp.sum(as_float, axis=1), jnp.sum(as_float * as_float, axis=1)...  18.1 us
  transfers between devices with their start and end apart: 4, of which 4 were waited for; matrix products, arithmetic and copies ran while one was open for 0% of the time, Pallas kernels for 0%

commit v1 on v0

--- a/solution.py
+++ b/solution.py
@@ -34,7 +34,7 @@
     hidden = jax.nn.gelu(preact + hidden_bias[None, :], approximate=False).astype(jnp.bfloat16)
     terms = jnp.dot(
         hidden,
-        lax.all_gather(weight_out, "rows", axis=1, tiled=True),
+        jnp.concatenate(lax.all_gather(weight_out, "rows"), axis=1),
         preferred_element_type=jnp.float32,
     )
     branch = lax.psum_scatter(terms, "mp", scatter_dimension=1, tiled=True)

time: 561 us -> 531 us (0.947)
  waiting for transfers between devices: 467 us -> 384 us
  local copies, waits for them, and re-layouts: 2.31 us -> 51.4 us
    reshape x0 -> x1, local copies, waits for them, and re-layouts: none -> 49.1 us  [body(): jnp.concatenate(lax.all_gather(weight_out, 'rows'), axis=1)]
    reduce_scatter x1, waiting for transfers between devices: 67 us -> 24 us  [body(): lax.psum_scatter(jnp.dot(shuffled, weight_in, preferred_element_type=jnp....]
    all_gather x1, waiting for transfers between devices: 335 us -> 295 us  [body(): lax.all_gather(weight_out, 'rows')]
  transfers between devices with their start and end apart: 4 -> 4, of which waited for: 4 -> 4; matrix products, arithmetic and copies ran while one was open for 0% -> 12% of each run, Pallas kernels for 0% -> 0%
where the time goes in v1:
time: 531 us; the launch traced here: 530 us
  waiting for transfers between devices  384 us (72%)
  local copies, waits for them, and re-layouts  51.4 us (10%)
  blocking collectives  44.5 us (8%)
  matrix products  32.3 us (6%)
  between operations  13.1 us (2%)
    all_gather x1, waiting for transfers between devices, body(): lax.all_gather(weight_out, 'rows')  295 us
    reshape x1, local copies, waits for them, and re-layouts, body(): jnp.concatenate(lax.all_gather(weight_out, 'rows'), axis=1)  49.1 us
    reduce_scatter x1, waiting for transfers between devices, body(): branch = lax.psum_scatter(terms, 'mp', scatter_dimension=1, tiled=True)  40.5 us
    all_to_all x1, blocking collectives, body(): lax.all_to_all(normed, 'rows', split_axis=1, concat_axis=0, tiled=True)  26.5 us
    reduce_scatter x1, waiting for transfers between devices, body(): lax.psum_scatter(jnp.dot(shuffled, weight_in, preferred_element_type=jnp....  24 us
    all_gather x1, waiting for transfers between devices, body(): normed = lax.all_gather(shard_norm, 'mp', axis=1, tiled=True)  22.8 us
    dot_general x1, matrix products, body(): jnp.dot(hidden, jnp.concatenate(lax.all_gather(weight_out, 'rows'), axis=...  21.6 us
    psum x1, blocking collectives, body(): lax.psum((jnp.sum(as_float, axis=1), jnp.sum(as_float * as_float, axis=1)...  18.1 us
  transfers between devices with their start and end apart: 4, of which 4 were waited for; matrix products, arithmetic and copies ran while one was open for 12% of the time, Pallas kernels for 0%

profile of v1, /device:TPU:0, one launch (start us, length us, event | category | flops | bytes accessed | tf_op | source)
XLA Modules:
  0.0 529.6 jit_solution(4487441406624949564)
XLA Ops:
  6.5 0.0 all-gather.4.cloned.1.call-start
  6.5 1.1 convert_reduce_fusion
  7.6 0.8 dynamic_slice.3
  8.4 18.1 %all-reduce = (f32[128]{0:T(128)S(1)}, f32[128]{0:T(128)S(1)}) all-reduce(f32[128]{0:T(128)S(1)} %get-tuple-element.6, f32[128]{0:T(128)S(1)} %get-tuple-element.5), channel_id=1, replica_groups=mesh['rows'=4,'mp'=8] {'mp'}, use_global_device_ids=true, to_apply=%region_3.0 | all-reduce | flops 256 | bytes 2048 | tf_op jit(solution)/shard_map/psum | solution.py:19
  26.5 1.8 fusion.45
  28.2 0.0 all-gather.4.cloned.1.call-update
  28.3 0.0 all-gather.6.cloned.1.call-start
  28.3 0.7 all-gather.6.cloned.1.call-update
  29.0 0.0 reduce-scatter.3.cloned.1.call-start
  29.1 22.8 %all-gather.4.cloned.1.call-done = bf16[128,6144]{1,0:T(8,128)(2,1)} async-done(((bf16[128,768]{1,0:T(8,128)(2,1)}), bf16[128,6144]{1,0:T(8,128)(2,1)}) %all-gather.4.cloned.1.call-update) | async-done | bytes 1572880 | tf_op jit(solution)/shard_map/all_gather | solution.py:26
  51.9 1.5 copy.11
  53.4 26.5 %all_to_all.19 = bf16[128,4,1536]{2,0,1:T(8,128)(2,1)S(1)} all-to-all(bf16[128,4,1536]{2,0,1:T(8,128)(2,1)S(1)} %bitcast.16), channel_id=1, replica_groups=mesh['rows'=4,'mp'=8] {'rows'}, dimensions={1} | all-to-all | bytes 3145728 | tf_op jit(solution)/shard_map/all_to_all | solution.py:27
  79.9 10.7 %fusion.78 = f32[512,3072]{1,0:T(8,128)} fusion(bf16[512,1536]{1,0:T(8,128)(2,1)S(1)} %bitcast.18, bf16[1536,3072]{1,0:T(8,128)(2,1)} %param.8), kind=kOutput, calls=%fused_computation.93 | convolution fusion | flops 4831838208 | bytes 17301504 | tf_op jit(solution)/shard_map/dot_general | solution.py:29
  90.6 0.0 reduce-scatter.3.cloned.1.call-update
  90.6 0.0 reduce-scatter.5.cloned.1.call-start
  90.6 295.5 %all-gather.6.cloned.1.call-done = bf16[12288,1536]{1,0:T(8,128)(2,1)} async-done(((bf16[3072,1536]{1,0:T(8,128)(2,1)}), bf16[12288,1536]{1,0:T(8,128)(2,1)}) %all-gather.6.cloned.1.call-update) | async-done | bytes 37748752 | tf_op jit(solution)/shard_map/all_gather | solution.py:37
  386.1 0.0 copy-start.1
  386.1 49.1 %copy.8 = bf16[3072,4,1536]{0,2,1:T(8,128)(2,1)} copy(bf16[3072,4,1536]{2,0,1:T(8,128)(2,1)} %bitcast.14) | data formatting | bytes 75497472 | tf_op jit(solution)/shard_map/reshape | solution.py:37
  435.2 24.0 %reduce-scatter.3.cloned.1.call-done = f32[128,3072]{1,0:T(8,128)} async-done(((f32[512,3072]{1,0:T(8,128)}), f32[128,3072]{1,0:T(8,128)}) %reduce-scatter.3.cloned.1.call-update) | async-done | bytes 1572880 | tf_op jit(solution)/shard_map/reduce_scatter | solution.py:28
  459.2 0.0 copy-done.1
  459.2 21.6 %fusion.10 = f32[128,6144]{1,0:T(8,128)} fusion(bf16[3072,6144]{0,1:T(8,128)(2,1)} %bitcast.15, f32[128,3072]{1,0:T(8,128)} %reduce-scatter.3.cloned.1.call-done, f32[3072]{0:T(1024)S(1)} %copy-done.1), kind=kOutput, calls=%fused_computation.20 | convolution fusion | flops 4857790464 | bytes 42479616 | tf_op jit(solution)/shard_map/dot_general | solution.py:35
  480.8 0.0 copy-start
  480.8 0.0 reduce-scatter.5.cloned.1.call-update
  480.8 40.5 %reduce-scatter.5.cloned.1.call-done = f32[128,768]{1,0:T(8,128)} async-done(((f32[128,6144]{1,0:T(8,128)}), f32[128,768]{1,0:T(8,128)}) %reduce-scatter.5.cloned.1.call-update) | async-done | bytes 393232 | tf_op jit(solution)/shard_map/reduce_scatter | solution.py:40
  521.4 0.0 copy-done
  521.4 1.7 fusion.47
  (1 shorter events, 0.0 us)
Async XLA Ops:
  6.5 45.4 %all-gather.4.cloned.1.call-start = ((), (), s32[]{:S(2)}) async-start(), calls=%async_computation.3 | async-start | bytes 1769472 | tf_op jit(solution)/shard_map/all_gather | solution.py:26
  28.3 357.9 %all-gather.6.cloned.1.call-start = ((), (), s32[]{:S(2)}) async-start(), calls=%async_computation.6 | async-start | bytes 47185920 | tf_op jit(solution)/shard_map/all_gather | solution.py:37
  29.0 430.2 %reduce-scatter.3.cloned.1.call-start = ((), (), s32[]{:S(2)}) async-start(), calls=%async_computation.4 | async-start | bytes 7864320 | tf_op jit(solution)/shard_map/reduce_scatter | solution.py:28
  90.6 430.8 %reduce-scatter.5.cloned.1.call-start = ((), (), s32[]{:S(2)}) async-start(), calls=%async_computation.5 | async-start | bytes 3538944 | tf_op jit(solution)/shard_map/reduce_scatter | solution.py:40
  386.1 73.0 %copy-start.1 = (f32[3072]{0:T(1024)S(1)}, f32[3072]{0:T(1024)}, u32[]{:S(2)}) copy-start(f32[3072]{0:T(1024)} %param.7) | copy-start | bytes 36868
  480.8 40.6 %copy-start = (bf16[128,768]{1,0:T(8,128)(2,1)S(1)}, bf16[128,768]{1,0:T(8,128)(2,1)}, u32[]{:S(2)}) copy-start(bf16[128,768]{1,0:T(8,128)(2,1)} %param.5) | copy-start | bytes 589828
Sparse Core Ops, SparseCore 0:
  28.4 23.4 all-gather.3
  53.8 332.3 all-gather.5
  389.1 70.0 reduce-scatter.2
  481.0 40.3 reduce-scatter.4
